TPU v7x, 32 devices: a whole 2x2x4 slice. The times are simulated.
32 devices in a mesh: ta: 2 (over core), gx: 16 (over z, y, x).
Axes of the slice: x: 2, y: 2, z: 4, core: 2. Of those that a mesh axis runs over, the one named last changes fastest.
Arguments:
- time_links: float32 [6, 2, 3, 3, 96, 4608], P('ta', None, None, None, 'gx'), may hold values from -1 to 1, as said below
Outputs:
- loop_planes: float32 [96, 2, 4608], P('gx', None, 'ta')
- correlator: float32 [96, 49], P('gx')
Inputs may be any that keep to these rules, and one draw needn't show every extreme that they name: At every site and time, the matrix time_links[t, 0] + i time_links[t, 1] is special unitary.
All inputs are finite; a program needn't handle non-finite values.
Results may differ from a plain program's by a relative error of at most 0.00029.
Values sent between devices are 32-bit elements; how exact they have to be, the bound alone decides.
A program may use at most 64 MiB of HBM per device.

v0:
```python
import functools

import jax
import jax.numpy as jnp
from jax import lax
from jax.experimental import pallas as pl
from jax.experimental.pallas import tpu as pltpu
from jax.sharding import PartitionSpec as P

LANES = 128
SUBLANES = 8
MESH = pl.DeviceIdType.MESH


def cross_conj(first, second):
    row = []
    for k in range(3):
        a, b = (k + 1) % 3, (k + 2) % 3
        ar, ai = first[a]
        br, bi = first[b]
        cr, ci = second[a]
        dr, di = second[b]
        real = (ar * dr - ai * di) - (br * cr - bi * ci)
        imag = (br * ci + bi * cr) - (ar * di + ai * dr)
        row.append((real, imag))
    return row


def row_times(row, matrix):
    out = []
    for k in range(3):
        real = imag = None
        for m in range(3):
            ar, ai = row[m]
            br, bi = matrix[m][k]
            pr = ar * br - ai * bi
            pi = ar * bi + ai * br
            real = pr if real is None else real + pr
            imag = pi if imag is None else imag + pi
        out.append((real, imag))
    return out


def product_rows(load, slices):
    rows = [[load(0, r, c) for c in range(3)] for r in range(2)]
    for t in range(1, slices):
        matrix = [[load(t, r, c) for c in range(3)] for r in range(2)]
        matrix.append(cross_conj(matrix[0], matrix[1]))
        rows = [row_times(row, matrix) for row in rows]
    return rows


def trace_of_product(left, right):
    left = left + [cross_conj(left[0], left[1])]
    right = right + [cross_conj(right[0], right[1])]
    real = imag = None
    for i in range(3):
        for j in range(3):
            ar, ai = left[i][j]
            br, bi = right[j][i]
            pr = ar * br - ai * bi
            pi = ar * bi + ai * br
            real = pr if real is None else real + pr
            imag = pi if imag is None else imag + pi
    return real / 3.0, imag / 3.0


def kernel(
    dims,
    x_ref,
    loop_ref,
    corr_ref,
    xin,
    psend,
    precv,
    tr,
    gath,
    gram,
    part,
    sel,
    in_sem,
    out_sem,
    s1,
    r1,
    s2,
    r2,
    s3,
    r3,
):
    slices, planes, sites, gx_n, chunks, reducers, longest = dims
    half = sites // 2
    chunk = half // chunks
    tiles = chunk // LANES
    per = 2 * half // LANES // reducers
    width = per * LANES
    rp = tr.shape[0]
    wide = gram.shape[1]
    ta = lax.axis_index("ta")
    gx = lax.axis_index("gx")
    other = 1 - ta
    mine = (gx * reducers + gx_n - 1) // gx_n
    is_reducer = jnp.logical_and(mine < reducers, (mine * gx_n) // reducers == gx)

    def in_copy(order, c, i):
        owner = other if order == 0 else ta
        start = pl.multiple_of(owner * half + c * chunk + i * LANES, LANES)
        slot = order * chunks + c
        return pltpu.make_async_copy(
            x_ref.at[:, pl.ds(0, 2), :, :, :, pl.ds(start, LANES)],
            xin.at[slot, :, :, :, :, i],
            in_sem.at[slot, i],
        )

    for order in range(2):
        for c in range(chunks):
            for i in range(tiles):
                in_copy(order, c, i).start()

    barrier = pltpu.get_barrier_semaphore()
    for core in range(2):

        def greet(j, carry, core=core):
            @pl.when(jnp.logical_or(core != ta, j != gx))
            def _():
                pl.semaphore_signal(barrier, inc=1, device_id={"ta": core, "gx": j}, device_id_type=MESH)

            return carry

        lax.fori_loop(0, gx_n, greet, 0)

    tr[...] = jnp.zeros(tr.shape, jnp.float32)

    flat = xin.reshape(*xin.shape[:4], planes * tiles * 2, LANES)

    def loader(slot, i):
        def load(t, r, c):
            return tuple(
                flat[slot, t, r, c, pl.ds(2 * i + q, planes, stride=2 * tiles), :]
                for q in range(2)
            )

        return load

    def far_chunk(c):
        for i in range(tiles):
            in_copy(0, c, i).wait()
        slot = c

        def tile(i, carry):
            lanes = pl.ds(pl.multiple_of(i * LANES, LANES), LANES)
            rows = product_rows(loader(slot, i), slices)
            for r in range(2):
                for k in range(3):
                    for q in range(2):
                        psend[slot, (r * 3 + k) * 2 + q, 0:planes, lanes] = rows[r][k][q]
            return carry

        lax.fori_loop(0, tiles, tile, 0)

    for c in range(chunks):
        far_chunk(c)

    pl.semaphore_wait(barrier, 2 * gx_n - 1)

    def swap(c):
        return pltpu.make_async_remote_copy(
            src_ref=psend.at[c],
            dst_ref=precv.at[c],
            send_sem=s1.at[c],
            recv_sem=r1.at[c],
            device_id={"ta": other, "gx": gx},
            device_id_type=MESH,
        )

    for c in range(chunks):
        swap(c).start()

    def scatter(k, target, sender):
        return pltpu.make_async_remote_copy(
            src_ref=tr.at[:, pl.ds(pl.multiple_of(k * width, LANES), width)],
            dst_ref=gath.at[sender],
            send_sem=s2.at[k],
            recv_sem=r2.at[sender],
            device_id={"ta": ta, "gx": target},
            device_id_type=MESH,
        )

    def out_copy(c, q):
        lanes = pl.ds(pl.multiple_of(q * half + c * chunk, LANES), chunk)
        return pltpu.make_async_copy(
            tr.at[:, lanes],
            loop_ref.at[:, lanes],
            out_sem.at[c * 2 + q],
        )

    def near_chunk(step):
        c = step
        for i in range(tiles):
            in_copy(1, c, i).wait()
        swap(c).wait_recv()

        def tile(i, carry):
            lanes = pl.ds(pl.multiple_of(i * LANES, LANES), LANES)
            rows = product_rows(loader(chunks + c, i), slices)
            theirs = [
                [
                    tuple(precv[c, (r * 3 + k) * 2 + q, 0:planes, lanes] for q in range(2))
                    for k in range(3)
                ]
                for r in range(2)
            ]
            pair = trace_of_product(rows, theirs)
            for q in range(2):
                place = pl.multiple_of(q * half + c * chunk + i * LANES, LANES)
                tr[0:planes, pl.ds(place, LANES)] = pair[q]
            return carry

        lax.fori_loop(0, tiles, tile, 0)
        for q in range(2):
            out_copy(c, q).start()
            for part_index in range(tiles // per):
                k = q * (reducers // 2) + c * (tiles // per) + part_index
                target = (k * gx_n) // reducers

                @pl.when(target != gx)
                def _():
                    scatter(k, target, gx).start()

                @pl.when(target == gx)
                def _():
                    lanes = pl.ds(pl.multiple_of(k * width, LANES), width)
                    gath[gx] = tr[:, lanes]

    for step in range(chunks):
        near_chunk(step)

    def select(i, carry):
        shape = (wide, sel.shape[2])
        column = lax.broadcasted_iota(jnp.int32, shape, 0)
        separation = lax.broadcasted_iota(jnp.int32, shape, 1)
        within = column % rp
        plane = planes * (column // rp) + within
        away = plane - (planes * gx + i + separation)
        hit = jnp.logical_or(away == 0, away == -planes * gx_n)
        hit = jnp.logical_and(hit, within < planes)
        sel[i] = jnp.where(hit, 1.0, 0.0).astype(jnp.bfloat16)
        return carry

    lax.fori_loop(0, planes, select, 0)

    def report(core, j, slot):
        return pltpu.make_async_remote_copy(
            src_ref=gram.at[pl.ds(pl.multiple_of(j * rp, SUBLANES), rp), :],
            dst_ref=part.at[slot],
            send_sem=s3.at[core * gx_n + j],
            recv_sem=r3.at[slot],
            device_id={"ta": core, "gx": j},
            device_id_type=MESH,
        )

    @pl.when(is_reducer)
    def _():
        def arrive(j, carry):
            @pl.when(j != gx)
            def _():
                scatter(0, gx, j).wait_recv()

            return carry

        lax.fori_loop(0, gx_n, arrive, 0)
        rows = gath[...].reshape(gx_n * rp, width)
        gram[...] = lax.dot_general(
            rows,
            rows,
            (((1,), (1,)), ((), ())),
            precision=lax.Precision.HIGHEST,
            preferred_element_type=jnp.float32,
        )
        slot = ta * reducers + mine
        for core in range(2):

            def tell(j, carry, core=core):
                @pl.when(jnp.logical_or(core != ta, j != gx))
                def _():
                    report(core, j, slot).start()

                return carry

            lax.fori_loop(0, gx_n, tell, 0)
        part[slot] = gram[pl.ds(pl.multiple_of(gx * rp, SUBLANES), rp), :]

    for core in range(2):

        def hear(k, carry, core=core):
            source = (k * gx_n) // reducers

            @pl.when(jnp.logical_or(core != ta, source != gx))
            def _():
                report(core, 0, core * reducers + k).wait_recv()

            return carry

        lax.fori_loop(0, reducers, hear, 0)

    total = jnp.sum(part[...], axis=0)
    high = total.astype(jnp.bfloat16).astype(jnp.float32)
    rest = total - high
    middle = rest.astype(jnp.bfloat16).astype(jnp.float32)
    low = rest - middle
    row_index = lax.broadcasted_iota(jnp.int32, total.shape, 0)
    answer = jnp.zeros((3 * rp, sel.shape[2]), jnp.float32)
    for i in range(planes):
        keep = row_index == i
        pieces = [jnp.where(keep, piece, 0.0) for piece in (high, middle, low)]
        stacked = jnp.concatenate(pieces, axis=0).astype(jnp.bfloat16)
        answer = answer + jnp.dot(stacked, sel[i], preferred_element_type=jnp.float32)
    answer = answer[0:rp] + answer[rp : 2 * rp] + answer[2 * rp : 3 * rp]
    corr_ref[...] = answer[0:planes, 0 : longest + 1] / sites

    for c in range(chunks):
        swap(c).wait_send()
        for q in range(2):
            out_copy(c, q).wait()

    def drain(k, carry):
        @pl.when((k * gx_n) // reducers != gx)
        def _():
            scatter(k, gx, gx).wait_send()

        return carry

    lax.fori_loop(0, reducers, drain, 0)

    @pl.when(is_reducer)
    def _():
        for core in range(2):

            def drain_report(j, carry, core=core):
                @pl.when(jnp.logical_or(core != ta, j != gx))
                def _():
                    report(core, j, 0).wait_send()

                return carry

            lax.fori_loop(0, gx_n, drain_report, 0)


def per_device(gx_n, time_links):
    slices, _, _, _, planes, sites = time_links.shape
    held = time_links.transpose(0, 2, 3, 4, 1, 5)
    half = sites // 2
    longest = planes * (gx_n // 2)
    blocks = half // LANES
    chunks = next(c for c in (6, 3, 1) if blocks % c == 0)
    tiles = blocks // chunks
    per = min(p for p in range(1, tiles + 1) if tiles % p == 0 and 2 * blocks // p <= gx_n)
    reducers = 2 * blocks // per
    rp = -(-planes // SUBLANES) * SUBLANES
    wide = gx_n * rp
    chunk = tiles * LANES
    far = -(-(longest + 1) // LANES) * LANES
    dims = (slices, planes, sites, gx_n, chunks, reducers, longest)
    dma = pltpu.SemaphoreType.DMA
    loops, correlator = pl.pallas_call(
        functools.partial(kernel, dims),
        out_shape=(
            jax.ShapeDtypeStruct((rp, sites), jnp.float32),
            jax.ShapeDtypeStruct((planes, longest + 1), jnp.float32),
        ),
        in_specs=[pl.BlockSpec(memory_space=pl.ANY)],
        out_specs=(
            pl.BlockSpec(memory_space=pl.ANY),
            pl.BlockSpec(memory_space=pltpu.VMEM),
        ),
        scratch_shapes=[
            pltpu.VMEM((2 * chunks + 1, slices, 2, 3, planes, tiles, 2, LANES), jnp.float32),
            pltpu.VMEM((chunks, 12, rp, chunk), jnp.float32),
            pltpu.VMEM((chunks, 12, rp, chunk), jnp.float32),
            pltpu.VMEM((rp, sites), jnp.float32),
            pltpu.VMEM((gx_n, rp, per * LANES), jnp.float32),
            pltpu.VMEM((wide, wide), jnp.float32),
            pltpu.VMEM((2 * reducers, rp, wide), jnp.float32),
            pltpu.VMEM((planes, wide, far), jnp.bfloat16),
            dma((2 * chunks, tiles)),
            dma((2 * chunks,)),
            dma((chunks,)),
            dma((chunks,)),
            dma((reducers,)),
            dma((gx_n,)),
            dma((2 * gx_n,)),
            dma((2 * reducers,)),
        ],
        compiler_params=pltpu.CompilerParams(collective_id=0, has_side_effects=True),
    )(held)
    return loops[0:planes].reshape(planes, 2, half), correlator


def solution(mesh):
    in_specs = (P("ta", None, None, None, "gx", None),)
    out_specs = (P("gx", None, "ta"), P("gx", None))
    return jax.shard_map(
        functools.partial(per_device, mesh.shape["gx"]),
        mesh=mesh,
        in_specs=in_specs,
        out_specs=out_specs,
        check_vma=False,
    )
```

profile of v0, /device:TPU:0, one launch (start us, length us, event | category | flops | bytes accessed | tf_op | source)
XLA Modules:
  0.0 25.3 jit_solution(6435602445348603375)
XLA Ops:
  0.6 21.8 %shard_map.30 = (f32[8,4608]{1,0:T(8,128)}, f32[6,49]{1,0:T(8,128)}) custom-call(f32[3,3,3,6,2,4608]{5,4,3,2,1,0:T(2,128)} %bitcast.2), custom_call_target="tpu_custom_call" | custom-call | tf_op jit(solution)/shard_map/pallas_call | solution.py:364
  22.4 1.6 %reshape.7 = f32[6,2,2304]{2,1,0:T(2,128)} reshape(f32[6,4608]{1,0:T(8,128)} %bitcast.3) | data formatting | bytes 221184 | tf_op jit(solution)/shard_map/reshape | solution.py:395
  24.0 1.3 %copy.4 = f32[6,49]{1,0:T(8,128)} copy(f32[6,49]{1,0:T(8,128)} %get-tuple-element.9) | data formatting | bytes 2352
where the time goes:
time: 25.5 us; the launch traced here: 25.3 us
  Pallas kernels  21.8 us (85%)
  local copies, waits for them, and re-layouts  2.89 us (11%)
  between operations  0.64 us (3%)
    pallas_call x1, Pallas kernels, per_device(): pl.pallas_call(functools.partial(kernel, dims), out_shape=(jax.ShapeDtype...  21.8 us
    reshape x1, local copies, waits for them, and re-layouts, per_device(): return (loops[0:planes].reshape(planes, 2, half), correlator)  1.63 us
    unnamed x1, local copies, waits for them, and re-layouts  1.26 us

commit v1 on v0

v1 whole, which is shorter than its diff:
```python
import functools

import jax
import jax.numpy as jnp
from jax import lax
from jax.experimental import pallas as pl
from jax.experimental.pallas import tpu as pltpu
from jax.sharding import PartitionSpec as P

LANES = 128
SUBLANES = 8
PARTS = 2
REDUCERS = 2 * 2 * PARTS
MESH = pl.DeviceIdType.MESH


def scope(name):
    return jax.named_scope(name)


def cross_conj(first, second):
    row = []
    for k in range(3):
        a, b = (k + 1) % 3, (k + 2) % 3
        ar, ai = first[a]
        br, bi = first[b]
        cr, ci = second[a]
        dr, di = second[b]
        real = (ar * dr - ai * di) - (br * cr - bi * ci)
        imag = (br * ci + bi * cr) - (ar * di + ai * dr)
        row.append((real, imag))
    return row


def row_times(row, matrix):
    out = []
    for k in range(3):
        real = imag = None
        for m in range(3):
            ar, ai = row[m]
            br, bi = matrix[m][k]
            pr = ar * br - ai * bi
            pi = ar * bi + ai * br
            real = pr if real is None else real + pr
            imag = pi if imag is None else imag + pi
        out.append((real, imag))
    return out


def product_rows(load, slices):
    rows = [[load(0, r, c) for c in range(3)] for r in range(2)]
    for t in range(1, slices):
        matrix = [[load(t, r, c) for c in range(3)] for r in range(2)]
        matrix.append(cross_conj(matrix[0], matrix[1]))
        rows = [row_times(row, matrix) for row in rows]
    return rows


def trace_of_product(left, right):
    right = right + [cross_conj(right[0], right[1])]
    real = imag = None
    for i in range(3):
        for j in range(3):
            ar, ai = left[i][j]
            br, bi = right[j][i]
            pr = ar * br - ai * bi
            pi = ar * bi + ai * br
            real = pr if real is None else real + pr
            imag = pi if imag is None else imag + pi
    return real / 3.0, imag / 3.0


def lateness(g):
    return g % 2 + g // 2 % 2 + g // 4


def kernel(
    dims,
    x_ref,
    loop_ref,
    corr_ref,
    xin,
    psend,
    precv,
    held,
    tr,
    gath,
    gram,
    part,
    in_sem,
    s1,
    r1,
    s2,
    r2,
    s3,
    r3,
    ready,
    partner,
):
    slices, planes, sites, gx_n, tiles, longest = dims
    rows = planes * tiles
    slab = planes // 2
    wide = planes * gx_n
    lane_tiles = gram.shape[0]
    groups = -(-rows // SUBLANES)
    cut = groups // 2
    ta = lax.axis_index("ta")
    gx = lax.axis_index("gx")
    other = 1 - ta
    base = gx_n // 4
    step = gx_n // 2 // REDUCERS
    mine = (gx - base) // step
    is_reducer = jnp.logical_and(
        jnp.logical_and(ta == 1, gx >= base),
        jnp.logical_and((gx - base) % step == 0, gx < base + REDUCERS * step),
    )
    from_part = mine % 2
    from_core = mine // 2 % 2
    from_comp = mine // 4
    late = lateness(gx)

    def home(h, q, core):
        return base + (q * 4 + core * 2 + h) * step

    def in_copy(order, h):
        owner = other if order == 0 else ta
        return pltpu.make_async_copy(
            x_ref.at[:, pl.ds(0, 2), :, :, pl.ds((owner * PARTS + h) * tiles, tiles)],
            xin.at[order * PARTS + h],
            in_sem.at[order * PARTS + h],
        )

    for order in range(2):
        for h in range(PARTS):
            in_copy(order, h).start()

    barrier = pltpu.get_barrier_semaphore()

    def arrive(semaphore, core, j):
        pl.semaphore_signal(semaphore, inc=1, device_id={"ta": core, "gx": j}, device_id_type=MESH)

    @pl.when(ta == 1)
    def _():
        arrive(barrier, 0, gx)

    expected = jnp.where(ta == 0, 1, 0)
    for h in range(PARTS):
        for q in range(2):
            place = home(h, q, ta)
            sooner = lateness(place) <= late

            @pl.when(jnp.logical_not(sooner))
            def _():
                arrive(barrier, 1, place)

            counts = jnp.logical_and(sooner, place != gx)
            expected = expected + jnp.where(counts, 1, 0)

    @pl.when(is_reducer)
    def _():
        def greet(j, carry):
            @pl.when(jnp.logical_and(late <= lateness(j), j != gx))
            def _():
                arrive(barrier, from_core, j)

            return carry

        lax.fori_loop(0, gx_n, greet, 0)

    before = jnp.int32(0)
    for j in range(gx_n):
        before = before + jnp.where(lateness(j) < late, 1, 0)
    expected = expected + jnp.where(is_reducer, before, 0)
    with scope("barrier"):

        @pl.when(expected > 0)
        def _():
            pl.semaphore_wait(barrier, expected)

    @pl.when(ta == 0)
    def _():
        arrive(partner, 1, gx)

    @pl.when(is_reducer)
    def _():
        def reply(j, carry):
            @pl.when(lateness(j) < late)
            def _():
                arrive(ready.at[from_part * 2 + from_comp], from_core, j)

            return carry

        lax.fori_loop(0, gx_n, reply, 0)

    flat_in = xin.reshape(*xin.shape[:4], rows * 2, LANES)
    flat_send = psend.reshape(PARTS, 12, rows, LANES)
    flat_recv = precv.reshape(PARTS, 12, rows, LANES)
    flat_loop = loop_ref.reshape(PARTS, rows * 2, LANES)
    flat_tr = tr.reshape(PARTS, 2, rows, LANES)
    flat_gath = gath.reshape(gx_n * rows, LANES)

    def loader(slot, start):
        def load(t, r, c):
            return tuple(
                flat_in[slot, t, r, c, pl.ds(2 * start + q, SUBLANES, stride=2), :]
                for q in range(2)
            )

        return load

    def begin(g):
        return jnp.minimum(g * SUBLANES, rows - SUBLANES)

    def swap(h, p):
        span = pl.ds(0, cut * SUBLANES // 2) if p == 0 else pl.ds(cut * SUBLANES // 2, rows // 2 - cut * SUBLANES // 2)
        return pltpu.make_async_remote_copy(
            src_ref=psend.at[h, :, span],
            dst_ref=precv.at[h, :, span],
            send_sem=s1.at[h * 2 + p],
            recv_sem=r1.at[h * 2 + p],
            device_id={"ta": other, "gx": gx},
            device_id_type=MESH,
        )

    pieces = ((0, cut), (cut, groups))

    for h in range(PARTS):
        with scope(f"farwait{h}"):
            in_copy(0, h).wait()
        for p, (low, high) in enumerate(pieces):
            def far(g, carry, h=h):
                start = begin(g)
                product = product_rows(loader(h, start), slices)
                for r in range(2):
                    for k in range(3):
                        for q in range(2):
                            flat_send[h, (r * 3 + k) * 2 + q, pl.ds(start, SUBLANES), :] = product[r][k][q]
                return carry

            with scope(f"far{h}{p}"):
                lax.fori_loop(low, high, far, 0)
            if h == 0 and p == 0:
                @pl.when(ta == 1)
                def _():
                    with scope("partner"):
                        pl.semaphore_wait(partner, 1)
            swap(h, p).start()

    for h in range(PARTS):
        with scope(f"nearwait{h}"):
            in_copy(1, h).wait()

        def near(g, carry, h=h):
            start = begin(g)
            product = product_rows(loader(PARTS + h, start), slices)
            product.append(cross_conj(product[0], product[1]))
            for r in range(3):
                for k in range(3):
                    for q in range(2):
                        held[h, (r * 3 + k) * 2 + q, pl.ds(start, SUBLANES), :] = product[r][k][q]
            return carry

        with scope(f"near{h}"):
            lax.fori_loop(0, groups, near, 0)

    def scatter(h, q, place):
        return pltpu.make_async_remote_copy(
            src_ref=tr.at[h, q],
            dst_ref=gath.at[gx],
            send_sem=s2,
            recv_sem=r2,
            device_id={"ta": 1, "gx": place},
            device_id_type=MESH,
        )

    for h in range(PARTS):
        for p, (low, high) in enumerate(pieces):
            with scope(f"swapwait{h}{p}"):
                swap(h, p).wait_recv()

            def trace(g, carry, h=h):
                start = begin(g)
                ours = [
                    [
                        tuple(held[h, (r * 3 + k) * 2 + q, pl.ds(start, SUBLANES), :] for q in range(2))
                        for k in range(3)
                    ]
                    for r in range(3)
                ]
                theirs = [
                    [
                        tuple(flat_recv[h, (r * 3 + k) * 2 + q, pl.ds(start, SUBLANES), :] for q in range(2))
                        for k in range(3)
                    ]
                    for r in range(2)
                ]
                pair = trace_of_product(ours, theirs)
                for q in range(2):
                    flat_loop[h, pl.ds(2 * start + q, SUBLANES, stride=2), :] = pair[q]
                    flat_tr[h, q, pl.ds(start, SUBLANES), :] = pair[q]
                return carry

            with scope(f"trace{h}{p}"):
                lax.fori_loop(low, high, trace, 0)
        for q in range(2):
            place = home(h, q, ta)
            itself = jnp.logical_and(ta == 1, place == gx)

            @pl.when(lateness(place) > late)
            def _():
                with scope(f"ready{h}{q}"):
                    pl.semaphore_wait(ready.at[h * 2 + q], 1)

            @pl.when(jnp.logical_not(itself))
            def _():
                scatter(h, q, place).start()

            @pl.when(itself)
            def _():
                gath[gx] = tr[h, q]

    def report(core, j, slot):
        return pltpu.make_async_remote_copy(
            src_ref=gram.at[:, pl.ds(j * slab, slab)],
            dst_ref=part.at[slot],
            send_sem=s3,
            recv_sem=r3,
            device_id={"ta": core, "gx": j},
            device_id_type=MESH,
        )

    def total(ref, semaphore):
        return pltpu.make_async_copy(ref, ref, semaphore)

    @pl.when(is_reducer)
    def _():
        with scope("gather"):
            @pl.when(from_core == 0)
            def _():
                total(gath, r2).wait()

            @pl.when(from_core == 1)
            def _():
                total(gath.at[pl.ds(0, gx_n - 1)], r2).wait()

        with scope("gram"):
            highs, lows = [], []
            for i in range(tiles):
                values = flat_gath[pl.ds(i, wide, stride=tiles), :]
                high = values.astype(jnp.bfloat16)
                highs.append(high)
                lows.append((values - high.astype(jnp.float32)).astype(jnp.bfloat16))
            high = jnp.concatenate(highs, axis=1)
            low = jnp.concatenate(lows, axis=1)

            def dot(a, b):
                return lax.dot_general(a, b, (((1,), (1,)), ((), ())), preferred_element_type=jnp.float32)

            product = dot(high, high) + (dot(high, low) + dot(low, high))
            padding = lane_tiles * LANES - wide
            if padding:
                product = jnp.concatenate([product, jnp.zeros((wide, padding), jnp.float32)], axis=1)
            flat_gram = gram.reshape(lane_tiles, wide, LANES)
            for i in range(lane_tiles):
                flat_gram[i] = product[:, i * LANES : (i + 1) * LANES]
        with scope("report"):
            for core in range(2):

                def tell(j, carry, core=core):
                    @pl.when(jnp.logical_or(core != ta, j != gx))
                    def _():
                        report(core, j, mine).start()

                    return carry

                lax.fori_loop(0, gx_n, tell, 0)
            part[mine] = gram[:, pl.ds(gx * slab, slab)]
        with scope("hear_r"):
            total(part.at[pl.ds(0, REDUCERS - 1)], r3).wait()

    @pl.when(jnp.logical_not(is_reducer))
    def _():
        with scope("hear"):
            total(part, r3).wait()

    sc = scope("final")
    sc.__enter__()
    flat_part = part.reshape(REDUCERS, lane_tiles, planes, LANES)
    chunks = []
    for i in range(lane_tiles):
        chunk = flat_part[0, i]
        for slot in range(1, REDUCERS):
            chunk = chunk + flat_part[slot, i]
        chunks.append(chunk)
    summed = chunks[0] if lane_tiles == 1 else jnp.concatenate(chunks, axis=1)
    extra = -planes % SUBLANES
    if extra:
        summed = jnp.concatenate([summed, jnp.zeros((extra, summed.shape[1]), jnp.float32)], axis=0)
    width = summed.shape[1]
    row_index = lax.broadcasted_iota(jnp.int32, summed.shape, 0)
    column = lax.broadcasted_iota(jnp.int32, summed.shape, 1)
    answer = jnp.zeros(summed.shape, jnp.float32)
    for i in range(planes):
        start = gx * planes + i
        ahead = pltpu.roll(summed, (width - start) % width, 1)
        if width == wide:
            value = ahead
        else:
            around = pltpu.roll(summed, (width + wide - start) % width, 1)
            value = jnp.where(column + start < wide, ahead, around)
        answer = jnp.where(row_index == i, value, answer)
    corr_ref[...] = answer[0:planes, 0 : longest + 1] / sites
    sc.__exit__(None, None, None)

    sc = scope("drain")
    sc.__enter__()
    for h in range(PARTS):
        for p in range(2):
            swap(h, p).wait_send()

    inside = jnp.logical_and(is_reducer, from_core == 1)
    sent = tr.reshape(PARTS * 2, rows // 2, 2, LANES)

    @pl.when(inside)
    def _():
        total(sent.at[pl.ds(0, 3)], s2).wait()

    @pl.when(jnp.logical_not(inside))
    def _():
        total(sent, s2).wait()

    @pl.when(is_reducer)
    def _():
        count = (2 * gx_n - 1) * slab * lane_tiles
        total(gath.reshape(gx_n * rows // 2, 2, LANES).at[pl.ds(0, count)], s3).wait()

    sc.__exit__(None, None, None)


def place_outputs(loop_in, corr_in, loop_out, corr_out, semaphores):
    tiles = loop_in.shape[2]
    copies = [pltpu.make_async_copy(corr_in, corr_out, semaphores.at[PARTS])]
    for h in range(PARTS):
        copies.append(
            pltpu.make_async_copy(
                loop_in.at[h], loop_out.at[:, pl.ds(h * tiles, tiles)], semaphores.at[h]
            )
        )
    for copy in copies:
        copy.start()
    for copy in copies:
        copy.wait()


def per_device(gx_n, time_links):
    slices, _, _, _, planes, sites = time_links.shape
    blocks = sites // LANES
    held = time_links.transpose(0, 2, 3, 4, 1, 5)
    held = held.reshape(slices, 3, 3, planes, 2, blocks, LANES).swapaxes(4, 5)
    tiles = blocks // 2 // PARTS
    rows = planes * tiles
    longest = planes * (gx_n // 2)
    wide = planes * gx_n
    lane_tiles = -(-wide // LANES)
    dims = (slices, planes, sites, gx_n, tiles, longest)
    dma = pltpu.SemaphoreType.DMA
    f32 = jnp.float32
    loops, correlator = pl.pallas_call(
        functools.partial(kernel, dims),
        out_shape=(
            pltpu.VMEM((PARTS, planes, tiles, 2, LANES), f32),
            pltpu.VMEM((planes, longest + 1), f32),
        ),
        in_specs=[pl.BlockSpec(memory_space=pl.ANY)],
        out_specs=(
            pl.BlockSpec(memory_space=pltpu.VMEM),
            pl.BlockSpec(memory_space=pltpu.VMEM),
        ),
        scratch_shapes=[
            pltpu.VMEM((2 * PARTS, slices, 2, 3, planes, tiles, 2, LANES), f32),
            pltpu.VMEM((PARTS, 12, rows // 2, 2, LANES), f32),
            pltpu.VMEM((PARTS, 12, rows // 2, 2, LANES), f32),
            pltpu.VMEM((PARTS, 18, rows, LANES), f32),
            pltpu.VMEM((PARTS, 2, rows // 2, 2, LANES), f32),
            pltpu.VMEM((gx_n, rows // 2, 2, LANES), f32),
            pltpu.VMEM((lane_tiles, wide // 2, 2, LANES), f32),
            pltpu.VMEM((REDUCERS, lane_tiles, planes // 2, 2, LANES), f32),
            dma((2 * PARTS,)),
            dma((2 * PARTS,)),
            dma((2 * PARTS,)),
            dma,
            dma,
            dma,
            dma,
            pltpu.SemaphoreType.REGULAR((2 * PARTS,)),
            pltpu.SemaphoreType.REGULAR,
        ],
        compiler_params=pltpu.CompilerParams(collective_id=0, has_side_effects=True),
    )(held)
    loops = pltpu.with_memory_space_constraint(loops, pltpu.VMEM)
    correlator = pltpu.with_memory_space_constraint(correlator, pltpu.VMEM)
    loops, correlator = pl.pallas_call(
        place_outputs,
        out_shape=(
            jax.ShapeDtypeStruct((planes, blocks // 2, 2, LANES), f32),
            jax.ShapeDtypeStruct((planes, longest + 1), f32),
        ),
        in_specs=[pl.BlockSpec(memory_space=pltpu.VMEM)] * 2,
        out_specs=(pl.BlockSpec(memory_space=pl.ANY),) * 2,
        scratch_shapes=[dma((PARTS + 1,))],
    )(loops, correlator)
    return loops.swapaxes(1, 2).reshape(planes, 2, sites // 2), correlator


def solution(mesh):
    in_specs = (P("ta", None, None, None, "gx", None),)
    out_specs = (P("gx", None, "ta"), P("gx", None))
    return jax.shard_map(
        functools.partial(per_device, mesh.shape["gx"]),
        mesh=mesh,
        in_specs=in_specs,
        out_specs=out_specs,
        check_vma=False,
    )
```

time: 25.5 us -> 17.2 us (0.67)
  Pallas kernels: 21.8 us -> 16.4 us
  local copies, waits for them, and re-layouts: 2.89 us -> 0 us
    pallas_call x1 -> x2, Pallas kernels: 21.8 us -> 16.4 us  [the longest x1 15.7 us: per_device(): pl.pallas_call(functools.partial(kernel, dims), out_shape=(pltpu.VMEM((PA...]
    reshape x1 -> x0, local copies, waits for them, and re-layouts: 1.63 us -> none  [per_device(): return (loops[0:planes].reshape(planes, 2, half), correlator)]
    unnamed x1 -> x0, local copies, waits for them, and re-layouts: 1.26 us -> none
where the time goes in v1:
time: 17.2 us; the launch traced here: 17 us
  Pallas kernels  16.4 us (95%)
  between operations  0.64 us (4%)
    pallas_call x1, Pallas kernels, per_device(): pl.pallas_call(functools.partial(kernel, dims), out_shape=(pltpu.VMEM((PA...  15.7 us
    pallas_call x1, Pallas kernels, per_device(): pl.pallas_call(place_outputs, out_shape=(jax.ShapeDtypeStruct((planes, bl...  0.67 us

profile of v1, /device:TPU:0, one launch (start us, length us, event | category | flops | bytes accessed | tf_op | source)
XLA Modules:
  0.0 17.0 jit_solution(5630948998960770101)
XLA Ops:
  0.6 15.7 %shard_map.30 = (f32[2,6,9,2,128]{4,3,2,1,0:T(2,128)S(1)}, f32[6,49]{1,0:T(8,128)S(1)}) custom-call(f32[3,3,3,6,36,2,128]{6,5,4,3,2,1,0:T(2,128)} %bitcast.8), custom_call_target="tpu_custom_call" | custom-call | tf_op jit(solution)/shard_map/pallas_call | solution.py:468
  16.4 0.7 %shard_map.31 = (f32[6,18,2,128]{3,2,1,0:T(2,128)}, f32[6,49]{1,0:T(8,128)}) custom-call(f32[2,6,9,2,128]{4,3,2,1,0:T(2,128)S(1)} %get-tuple-element.6.loop_in, f32[6,49]{1,0:T(8,128)S(1)} %get-tuple-element.7.corr_in), custom_call_target="tpu_custom_call" | custom-call | tf_op jit(solution)/shard_map/pallas_call | solution.py:502

commit v2 on v1

v2 whole, which is shorter than its diff:
```python
import functools

import jax
import jax.numpy as jnp
from jax import lax
from jax.experimental import pallas as pl
from jax.experimental.pallas import tpu as pltpu
from jax.sharding import PartitionSpec as P

LANES = 128
SUBLANES = 8
PARTS = 2
REDUCERS = 2 * 2 * PARTS
MESH = pl.DeviceIdType.MESH


def scope(name):
    return jax.named_scope(name)


def cross_conj(first, second):
    row = []
    for k in range(3):
        a, b = (k + 1) % 3, (k + 2) % 3
        ar, ai = first[a]
        br, bi = first[b]
        cr, ci = second[a]
        dr, di = second[b]
        real = (ar * dr - ai * di) - (br * cr - bi * ci)
        imag = (br * ci + bi * cr) - (ar * di + ai * dr)
        row.append((real, imag))
    return row


def row_times(row, matrix):
    out = []
    for k in range(3):
        real = imag = None
        for m in range(3):
            ar, ai = row[m]
            br, bi = matrix[m][k]
            pr = ar * br - ai * bi
            pi = ar * bi + ai * br
            real = pr if real is None else real + pr
            imag = pi if imag is None else imag + pi
        out.append((real, imag))
    return out


def product_rows(load, slices):
    rows = [[load(0, r, c) for c in range(3)] for r in range(2)]
    for t in range(1, slices):
        matrix = [[load(t, r, c) for c in range(3)] for r in range(2)]
        matrix.append(cross_conj(matrix[0], matrix[1]))
        rows = [row_times(row, matrix) for row in rows]
    return rows


def trace_of_product(left, right):
    right = right + [cross_conj(right[0], right[1])]
    real = imag = None
    for i in range(3):
        for j in range(3):
            ar, ai = left[i][j]
            br, bi = right[j][i]
            pr = ar * br - ai * bi
            pi = ar * bi + ai * br
            real = pr if real is None else real + pr
            imag = pi if imag is None else imag + pi
    return real / 3.0, imag / 3.0


def kernel(dims, split, x_ref, *refs):
    slices, planes, sites, gx_n, longest = dims
    count = len(split)
    refs = list(refs)

    def take(n):
        taken = refs[:n]
        del refs[:n]
        return taken

    loop_refs = take(count)
    (corr_ref,) = take(1)
    far_in, near_in = take(count), take(count)
    psend, precv, held, tr = take(count), take(count), take(count), take(count)
    gath = take(2)
    gram, part, in_sem, s1, r1, s2, r2, s3, r3, ready, partner, cleared = refs
    slab = planes // 2
    wide = planes * gx_n
    lane_tiles = gram.shape[0]
    ta = lax.axis_index("ta")
    gx = lax.axis_index("gx")
    other = 1 - ta
    half = sum(n for _, n in split)
    base = gx_n // 4
    step = gx_n // 2 // REDUCERS
    mine = (gx - base) // step
    is_home = jnp.logical_and(
        gx >= base,
        jnp.logical_and((gx - base) % step == 0, gx < base + REDUCERS * step),
    )
    is_reducer = jnp.logical_and(ta == 1, is_home)
    from_part = mine % 2
    from_core = mine // 2 % 2
    from_comp = mine // 4
    early = gx_n // 2 + gx_n // 4
    near_targets = gx_n // 4
    is_first = gx == 0

    def home(h, q, core):
        return base + (q * 4 + core * 2 + h) * step

    def in_copy(order, p):
        owner = other if order == 0 else ta
        start, n = split[p]
        return pltpu.make_async_copy(
            x_ref.at[:, pl.ds(0, 2), :, :, pl.ds(owner * half + start, n)],
            (far_in, near_in)[order][p],
            in_sem.at[order * count + p],
        )

    for order in range(2):
        for p in range(count):
            in_copy(order, p).start()

    barrier = pltpu.get_barrier_semaphore()

    def arrive(semaphore, core, j):
        pl.semaphore_signal(semaphore, inc=1, device_id={"ta": core, "gx": j}, device_id_type=MESH)

    @pl.when(ta == 1)
    def _():
        arrive(barrier, 0, gx)

    @pl.when(is_first)
    def _():
        for h in range(PARTS):
            for q in range(2):
                arrive(barrier, 0, home(h, q, ta))

    @pl.when(is_reducer)
    def _():
        for j in range(1, gx_n):

            @pl.when(j != gx)
            def _():
                arrive(barrier, 1, j)

    @pl.when(ta == 0)
    def _():
        with scope("join"):
            pl.semaphore_wait(barrier, jnp.where(is_home, 2, 1))
        arrive(partner, 1, gx)

        @pl.when(is_home)
        def _():
            arrive(ready.at[from_part * 2 + from_comp], from_core, 0)

    def clear():
        @pl.when(jnp.logical_and(ta == 1, jnp.logical_not(is_first)))
        def _():
            pl.semaphore_wait(barrier, jnp.where(is_home, REDUCERS - 1, REDUCERS))
            arrive(cleared, 0, gx)

        @pl.when(jnp.logical_and(ta == 0, jnp.logical_not(is_first)))
        def _():
            pl.semaphore_wait(cleared, 1)

    def rows_of(p):
        return planes * split[p][1]

    def begin(p, g):
        return jnp.minimum(g * SUBLANES, rows_of(p) - SUBLANES)

    def each_group(p, body):
        def run(g, carry):
            body(begin(p, g))
            return carry

        lax.fori_loop(0, -(-rows_of(p) // SUBLANES), run, 0)

    def loader(ref, rows, start):
        flat = ref.reshape(*ref.shape[:3], rows * 2, LANES)

        def load(t, r, c):
            return tuple(
                flat[t, r, c, pl.ds(2 * start + q, SUBLANES, stride=2), :] for q in range(2)
            )

        return load

    def flat_rows(ref):
        return ref.reshape(ref.shape[0], ref.shape[1] * 2, LANES)

    def swap(p):
        return pltpu.make_async_remote_copy(
            src_ref=psend[p],
            dst_ref=precv[p],
            send_sem=s1.at[p],
            recv_sem=r1.at[p],
            device_id={"ta": other, "gx": gx},
            device_id_type=MESH,
        )

    for p in range(count):
        with scope(f"farwait{p}"):
            in_copy(0, p).wait()

        def far(start, p=p):
            product = product_rows(loader(far_in[p], rows_of(p), start), slices)
            out = flat_rows(psend[p])
            for r in range(2):
                for k in range(3):
                    for q in range(2):
                        out[(r * 3 + k) * 2 + q, pl.ds(start, SUBLANES), :] = product[r][k][q]

        with scope(f"far{p}"):
            each_group(p, far)
        if p == 0:

            @pl.when(ta == 1)
            def _():
                with scope("partner"):
                    pl.semaphore_wait(partner, 1)

        swap(p).start()

    for p in range(count):
        with scope(f"nearwait{p}"):
            in_copy(1, p).wait()

        def near(start, p=p):
            product = product_rows(loader(near_in[p], rows_of(p), start), slices)
            product.append(cross_conj(product[0], product[1]))
            for r in range(3):
                for k in range(3):
                    for q in range(2):
                        held[p][(r * 3 + k) * 2 + q, pl.ds(start, SUBLANES), :] = product[r][k][q]

        with scope(f"near{p}"):
            each_group(p, near)

    def scatter(p, q, place):
        return pltpu.make_async_remote_copy(
            src_ref=tr[p].at[q],
            dst_ref=gath[p % 2].at[gx],
            send_sem=s2,
            recv_sem=r2.at[jnp.where(gx < early, 0, 2) + p % 2],
            device_id={"ta": 1, "gx": place},
            device_id_type=MESH,
        )

    def hand_over(p, q):
        place = home(p // 2, q, ta)
        itself = jnp.logical_and(ta == 1, place == gx)

        @pl.when(jnp.logical_not(itself))
        def _():
            scatter(p, q, place).start()

        @pl.when(itself)
        def _():
            gath[p % 2][gx] = tr[p][q]

    upper = jnp.where(gx < gx_n // 2, 1, 0)

    for p in range(count):
        with scope(f"swapwait{p}"):
            swap(p).wait_recv()

        def trace(start, p=p):
            theirs_ref = flat_rows(precv[p])

            def entry(ref, r, k):
                return tuple(ref[(r * 3 + k) * 2 + q, pl.ds(start, SUBLANES), :] for q in range(2))

            ours = [[entry(held[p], r, k) for k in range(3)] for r in range(3)]
            theirs = [[entry(theirs_ref, r, k) for k in range(3)] for r in range(2)]
            pair = trace_of_product(ours, theirs)
            flat_loop = loop_refs[p].reshape(rows_of(p) * 2, LANES)
            flat_tr = flat_rows(tr[p])
            for q in range(2):
                flat_loop[pl.ds(2 * start + q, SUBLANES, stride=2), :] = pair[q]
                flat_tr[q, pl.ds(start, SUBLANES), :] = pair[q]

        with scope(f"trace{p}"):
            each_group(p, trace)
        if p == 0:
            with scope("clear"):
                clear()

        @pl.when(jnp.logical_not(is_first))
        def _():
            hand_over(p, upper)
            hand_over(p, 1 - upper)

    @pl.when(is_first)
    def _():
        for h in range(PARTS):
            for q in range(2):
                with scope(f"ready{h}{q}"):
                    pl.semaphore_wait(ready.at[h * 2 + q], 1)
                for k in range(2):
                    hand_over(h * 2 + k, q)

    def report(core, j, slot):
        return pltpu.make_async_remote_copy(
            src_ref=gram.at[:, pl.ds(j * slab, slab)],
            dst_ref=part.at[slot],
            send_sem=s3,
            recv_sem=r3,
            device_id={"ta": core, "gx": j},
            device_id_type=MESH,
        )

    def total(ref, semaphore):
        return pltpu.make_async_copy(ref, ref, semaphore)

    flat_gram = gram.reshape(lane_tiles, wide, LANES)

    def contract(k, low, high, width):
        tiles = split[k][1]
        flat_gath = gath[k].reshape(gx_n * rows_of(k), LANES)
        tops, bottoms = [], []
        for i in range(tiles):
            values = flat_gath[pl.ds(i, width, stride=tiles), :]
            top = values.astype(jnp.bfloat16)
            tops.append(top)
            bottoms.append((values - top.astype(jnp.float32)).astype(jnp.bfloat16))
        top = jnp.concatenate(tops, axis=1)
        bottom = jnp.concatenate(bottoms, axis=1)

        def dot(a, b):
            return lax.dot_general(a, b, (((1,), (1,)), ((), ())), preferred_element_type=jnp.float32)

        return dot(top[low:high], top) + (dot(top[low:high], bottom) + dot(bottom[low:high], top))

    def place_rows(product, low, high, width):
        padding = lane_tiles * LANES - width
        if padding:
            product = jnp.concatenate([product, jnp.zeros((high - low, padding), jnp.float32)], axis=1)
        for i in range(lane_tiles):
            flat_gram[i, low:high] = product[:, i * LANES : (i + 1) * LANES]

    def tell(j, carry):
        for core in range(2):

            @pl.when(jnp.logical_or(core != ta, j != gx))
            def _():
                report(core, j, mine).start()

        return carry

    @pl.when(is_reducer)
    def _():
        first_rows = planes * near_targets
        products = []
        for k in range(2):
            with scope(f"gather0{k}"):
                @pl.when(from_core == 0)
                def _():
                    total(gath[k].at[pl.ds(0, early)], r2.at[k]).wait()

                @pl.when(from_core == 1)
                def _():
                    total(gath[k].at[pl.ds(0, early - 1)], r2.at[k]).wait()

            with scope(f"gram0{k}"):
                products.append(contract(k, 0, first_rows, planes * early))
        place_rows(products[0] + products[1], 0, first_rows, planes * early)
        with scope("report0"):
            lax.fori_loop(0, near_targets, tell, 0)
        products = []
        for k in range(2):
            with scope(f"gather1{k}"):
                total(gath[k].at[pl.ds(0, gx_n - early)], r2.at[2 + k]).wait()
            with scope(f"gram1{k}"):
                products.append(contract(k, first_rows, wide, wide))
        place_rows(products[0] + products[1], first_rows, wide, wide)
        with scope("report1"):
            lax.fori_loop(near_targets, gx_n, tell, 0)
            part[mine] = gram[:, pl.ds(gx * slab, slab)]
        with scope("hear_r"):
            total(part.at[pl.ds(0, REDUCERS - 1)], r3).wait()

    @pl.when(jnp.logical_not(is_reducer))
    def _():
        with scope("hear"):
            total(part, r3).wait()

    sc = scope("final")
    sc.__enter__()
    flat_part = part.reshape(REDUCERS, lane_tiles, planes, LANES)
    chunks = []
    for i in range(lane_tiles):
        chunk = flat_part[0, i]
        for slot in range(1, REDUCERS):
            chunk = chunk + flat_part[slot, i]
        chunks.append(chunk)
    summed = chunks[0] if lane_tiles == 1 else jnp.concatenate(chunks, axis=1)
    extra = -planes % SUBLANES
    if extra:
        summed = jnp.concatenate([summed, jnp.zeros((extra, summed.shape[1]), jnp.float32)], axis=0)
    width = summed.shape[1]
    row_index = lax.broadcasted_iota(jnp.int32, summed.shape, 0)
    column = lax.broadcasted_iota(jnp.int32, summed.shape, 1)
    answer = jnp.zeros(summed.shape, jnp.float32)
    for i in range(planes):
        start = gx * planes + i
        ahead = pltpu.roll(summed, (width - start) % width, 1)
        if width == wide:
            value = ahead
        else:
            around = pltpu.roll(summed, (width + wide - start) % width, 1)
            value = jnp.where(column + start < wide, ahead, around)
        answer = jnp.where(row_index == i, value, answer)
    corr_ref[...] = answer[0:planes, 0 : longest + 1] / sites
    sc.__exit__(None, None, None)

    sc = scope("drain")
    sc.__enter__()
    for p in range(count):
        swap(p).wait_send()

    inside = jnp.logical_and(is_reducer, from_core == 1)
    pool = gath[1].reshape(gx_n * rows_of(1) // 2, 2, LANES)
    message = planes * half // PARTS // 2

    @pl.when(inside)
    def _():
        total(pool.at[pl.ds(0, 3 * message)], s2).wait()

    @pl.when(jnp.logical_not(inside))
    def _():
        total(pool.at[pl.ds(0, 4 * message)], s2).wait()

    @pl.when(is_reducer)
    def _():
        left = (2 * gx_n - 1) * slab * lane_tiles
        while left:
            length = min(left, pool.shape[0])
            total(pool.at[pl.ds(0, length)], s3).wait()
            left -= length

    sc.__exit__(None, None, None)


def place_outputs(split, *refs):
    count = len(split)
    loop_in, (corr_in, loop_out, corr_out, semaphores) = refs[:count], refs[count:]
    copies = [pltpu.make_async_copy(corr_in, corr_out, semaphores.at[count])]
    for p, (start, n) in enumerate(split):
        copies.append(
            pltpu.make_async_copy(loop_in[p], loop_out.at[:, pl.ds(start, n)], semaphores.at[p])
        )
    for copy in copies:
        copy.start()
    for copy in copies:
        copy.wait()


def per_device(gx_n, time_links):
    slices, _, _, _, planes, sites = time_links.shape
    blocks = sites // LANES
    held = time_links.transpose(0, 2, 3, 4, 1, 5)
    held = held.reshape(slices, 3, 3, planes, 2, blocks, LANES).swapaxes(4, 5)
    half = blocks // 2
    tiles = half // PARTS
    small = tiles // 2
    split = []
    for h in range(PARTS):
        split += [(h * tiles, small), (h * tiles + small, tiles - small)]
    longest = planes * (gx_n // 2)
    wide = planes * gx_n
    lane_tiles = -(-wide // LANES)
    dims = (slices, planes, sites, gx_n, longest)
    dma = pltpu.SemaphoreType.DMA
    regular = pltpu.SemaphoreType.REGULAR
    f32 = jnp.float32
    count = len(split)
    links = [pltpu.VMEM((slices, 2, 3, planes, n, 2, LANES), f32) for _, n in split]
    swaps = [pltpu.VMEM((12, planes * n // 2, 2, LANES), f32) for _, n in split]
    scratch = links + links + swaps + swaps
    scratch += [pltpu.VMEM((18, planes * n, LANES), f32) for _, n in split]
    scratch += [pltpu.VMEM((2, planes * n // 2, 2, LANES), f32) for _, n in split]
    scratch += [pltpu.VMEM((gx_n, planes * n // 2, 2, LANES), f32) for _, n in split[:2]]
    scratch += [
        pltpu.VMEM((lane_tiles, wide // 2, 2, LANES), f32),
        pltpu.VMEM((REDUCERS, lane_tiles, planes // 2, 2, LANES), f32),
        dma((2 * count,)),
        dma((count,)),
        dma((count,)),
        dma,
        dma((4,)),
        dma,
        dma,
        regular((2 * PARTS,)),
        regular,
        regular,
    ]
    in_vmem = pl.BlockSpec(memory_space=pltpu.VMEM)
    results = pl.pallas_call(
        functools.partial(kernel, dims, split),
        out_shape=[pltpu.VMEM((planes, n, 2, LANES), f32) for _, n in split]
        + [pltpu.VMEM((planes, longest + 1), f32)],
        in_specs=[pl.BlockSpec(memory_space=pl.ANY)],
        out_specs=[in_vmem] * (count + 1),
        scratch_shapes=scratch,
        compiler_params=pltpu.CompilerParams(collective_id=0, has_side_effects=True),
    )(held)
    results = [pltpu.with_memory_space_constraint(r, pltpu.VMEM) for r in results]
    loops, correlator = pl.pallas_call(
        functools.partial(place_outputs, split),
        out_shape=(
            jax.ShapeDtypeStruct((planes, half, 2, LANES), f32),
            jax.ShapeDtypeStruct((planes, longest + 1), f32),
        ),
        in_specs=[in_vmem] * (count + 1),
        out_specs=(pl.BlockSpec(memory_space=pl.ANY),) * 2,
        scratch_shapes=[dma((count + 1,))],
    )(*results)
    return loops.swapaxes(1, 2).reshape(planes, 2, sites // 2), correlator


def solution(mesh):
    in_specs = (P("ta", None, None, None, "gx", None),)
    out_specs = (P("gx", None, "ta"), P("gx", None))
    return jax.shard_map(
        functools.partial(per_device, mesh.shape["gx"]),
        mesh=mesh,
        in_specs=in_specs,
        out_specs=out_specs,
        check_vma=False,
    )
```

time: 17.2 us -> 15.7 us (0.913)
  Pallas kernels: 16.4 us -> 14.9 us
    pallas_call x2, Pallas kernels: 16.4 us -> 14.9 us  [the longest x1 14.2 us: per_device(): pl.pallas_call(functools.partial(kernel, dims, split), out_shape=[pltpu.V...]
where the time goes in v2:
time: 15.7 us; the launch traced here: 15.5 us
  Pallas kernels  14.9 us (95%)
  between operations  0.64 us (4%)
    pallas_call x1, Pallas kernels, per_device(): pl.pallas_call(functools.partial(kernel, dims, split), out_shape=[pltpu.V...  14.2 us
    pallas_call x1, Pallas kernels, per_device(): pl.pallas_call(functools.partial(place_outputs, split), out_shape=(jax.Sh...  0.69 us

profile of v2, /device:TPU:0, one launch (start us, length us, event | category | flops | bytes accessed | tf_op | source)
XLA Modules:
  0.0 15.5 jit_solution(18441557182123862041)
XLA Ops:
  0.6 14.2 %shard_map.30 = (f32[6,4,2,128]{3,2,1,0:T(2,128)S(1)}, f32[6,5,2,128]{3,2,1,0:T(2,128)S(1)}, f32[6,4,2,128]{3,2,1,0:T(2,128)S(1)}, f32[6,5,2,128]{3,2,1,0:T(2,128)S(1)}, f32[6,49]{1,0:T(8,128)S(1)}) custom-call(f32[3,3,3,6,36,2,128]{6,5,4,3,2,1,0:T(2,128)} %bitcast.8), custom_call_target="tpu_custom_call" | custom-call | tf_op jit(solution)/shard_map/pallas_call | solution.py:503
  14.8 0.7 %shard_map.31 = (f32[6,18,2,128]{3,2,1,0:T(2,128)}, f32[6,49]{1,0:T(8,128)}) custom-call(f32[6,4,2,128]{3,2,1,0:T(2,128)S(1)} %get-tuple-element.9.refs_0_, f32[6,5,2,128]{3,2,1,0:T(2,128)S(1)} %get-tuple-element.10.refs_1_, f32[6,4,2,128]{3,2,1,0:T(2,128)S(1)} %get-tuple-element.11.refs_2_, f32[6,5,2,128]{3,2,1,0:T(2,128)S(1)} %get-tuple-element.12.refs_3_, ...), custom_call_target="tpu_custom_call" | custom-call | tf_op jit(solution)/shard_map/pallas_call | solution.py:513

commit v3 on v2

v3 whole, which is shorter than its diff:
```python
import functools

import jax
import jax.numpy as jnp
from jax import lax
from jax.experimental import pallas as pl
from jax.experimental.pallas import tpu as pltpu
from jax.sharding import PartitionSpec as P

LANES = 128
SUBLANES = 8
PARTS = 2
BITS = (4, 1, 2)
WALK = (0, 2, 1, 3)
REDUCERS = 2 * 2 * PARTS
MESH = pl.DeviceIdType.MESH


def cross_conj(first, second):
    row = []
    for k in range(3):
        a, b = (k + 1) % 3, (k + 2) % 3
        ar, ai = first[a]
        br, bi = first[b]
        cr, ci = second[a]
        dr, di = second[b]
        real = (ar * dr - ai * di) - (br * cr - bi * ci)
        imag = (br * ci + bi * cr) - (ar * di + ai * dr)
        row.append((real, imag))
    return row


def row_times(row, matrix):
    out = []
    for k in range(3):
        real = imag = None
        for m in range(3):
            ar, ai = row[m]
            br, bi = matrix[m][k]
            pr = ar * br - ai * bi
            pi = ar * bi + ai * br
            real = pr if real is None else real + pr
            imag = pi if imag is None else imag + pi
        out.append((real, imag))
    return out


def product_rows(load, slices):
    rows = [[load(r, c) for c in range(3)] for r in range(2)]
    for t in range(1, slices):
        matrix = [[load(2 * t + r, c) for c in range(3)] for r in range(2)]
        matrix.append(cross_conj(matrix[0], matrix[1]))
        rows = [row_times(row, matrix) for row in rows]
    return rows


def trace_of_product(left, right):
    right = right + [cross_conj(right[0], right[1])]
    real = imag = None
    for i in range(3):
        for j in range(3):
            ar, ai = left[i][j]
            br, bi = right[j][i]
            pr = ar * br - ai * bi
            pi = ar * bi + ai * br
            real = pr if real is None else real + pr
            imag = pi if imag is None else imag + pi
    return real / 3.0, imag / 3.0


def kernel(dims, split, x_ref, *refs):
    slices, planes, sites, gx_n, longest = dims
    count = len(split)
    refs = list(refs)

    def take(n):
        taken = refs[:n]
        del refs[:n]
        return taken

    loop_refs = take(count)
    (corr_ref,) = take(1)
    far_in = take(count)
    (near_pool,) = take(1)
    psend, precv, held, tr = take(count), take(count), take(count), take(count)
    gath = take(count)
    gram, part, in_sem, sent, r1, r2, r3, ready, beside = refs
    slab = planes // 2
    wide = planes * gx_n
    lane_tiles = gram.shape[0]
    ta = lax.axis_index("ta")
    gx = lax.axis_index("gx")
    other = 1 - ta
    half = sum(n for _, n in split)
    base = gx_n // 4
    step = gx_n // 2 // REDUCERS
    mine = (gx - base) // step
    is_home = jnp.logical_and(
        gx >= base,
        jnp.logical_and((gx - base) % step == 0, gx < base + REDUCERS * step),
    )
    is_reducer = jnp.logical_and(ta == 1, is_home)
    from_core, from_comp, from_part = (mine // bit % 2 for bit in BITS)
    from_part = 1 - from_part
    early = gx_n // 2 + gx_n // 4
    near_targets = gx_n // 4
    is_first = gx == 0
    is_slow = gx % 2 + gx // 2 % 2 + gx // 4 == 1

    half = sum(n for _, n in split)
    depth = near_pool.shape[0] // half
    near_in = [None] * count
    pairs = []
    place = 0
    for turn, p in enumerate(WALK):
        n = split[p][1]
        near_in[p] = near_pool.at[pl.ds(place * depth, n * depth)].reshape(
            depth // 3 // planes, 3, planes, n, 2, LANES
        )
        pairs += [(place, n)] if turn % 2 == 0 else []
        pairs[-1] = (pairs[-1][0], place + n - pairs[-1][0])
        place += n

    def home(h, q, core):
        return base + (core * BITS[0] + q * BITS[1] + (1 - h) * BITS[2]) * step

    def load_piece(order, p):
        owner = other if order == 0 else ta
        start, n = split[p]
        place = (far_in, near_in)[order][p]
        return pltpu.make_async_copy(
            x_ref.at[:, pl.ds(0, 2), :, :, pl.ds(owner * half + start, n)],
            place.reshape(slices, 2, *place.shape[1:]),
            in_sem.at[p if order == 0 else count + WALK.index(p) // 2],
        )

    def total(ref, semaphore):
        return pltpu.make_async_copy(ref, ref, semaphore)

    barrier = pltpu.get_barrier_semaphore()

    def arrive(semaphore, core, j):
        pl.semaphore_signal(semaphore, inc=1, device_id={"ta": core, "gx": j}, device_id_type=MESH)

    def greet():
        @pl.when(is_reducer)
        def _():
            for j in range(1, gx_n):

                @pl.when(j != gx)
                def _():
                    arrive(barrier, 1, j)

    greet()

    for order in range(2):
        for p in WALK:
            load_piece(order, p).start(priority=order)

    @pl.when(ta == 1)
    def _():
        arrive(barrier, 0, gx)

    @pl.when(is_first)
    def _():
        for h in range(PARTS):
            for q in range(2):
                arrive(barrier, 0, home(h, q, ta))

    @pl.when(ta == 0)
    def _():
        pl.semaphore_wait(barrier, jnp.where(is_home, 2, 1))
        arrive(beside, 1, gx)

        @pl.when(is_home)
        def _():
            arrive(ready.at[from_part * 2 + from_comp], from_core, 0)

    def clear():
        @pl.when(jnp.logical_and(ta == 1, jnp.logical_not(is_first)))
        def _():
            pl.semaphore_wait(barrier, jnp.where(is_home, REDUCERS - 1, REDUCERS))
            arrive(beside, 0, gx)

        @pl.when(jnp.logical_and(ta == 0, jnp.logical_not(is_first)))
        def _():
            pl.semaphore_wait(beside, 1)

    def rows_of(p):
        return planes * split[p][1]

    def begin(p, g):
        return jnp.minimum(g * SUBLANES, rows_of(p) - SUBLANES)

    def each_group(p, body):
        def run(g, carry):
            body(begin(p, g))
            return carry

        lax.fori_loop(0, -(-rows_of(p) // SUBLANES), run, 0)

    def loader(ref, rows, start):
        flat = ref.reshape(*ref.shape[:2], rows * 2, LANES)

        def load(i, c):
            return tuple(
                flat[i, c, pl.ds(2 * start + q, SUBLANES, stride=2), :] for q in range(2)
            )

        return load

    def flat_rows(ref):
        return ref.reshape(ref.shape[0], ref.shape[1] * 2, LANES)

    def swap(p):
        return pltpu.make_async_remote_copy(
            src_ref=psend[p],
            dst_ref=precv[p],
            send_sem=sent,
            recv_sem=r1.at[p],
            device_id={"ta": other, "gx": gx},
            device_id_type=MESH,
        )

    def do_far(p):
        load_piece(0, p).wait()

        def far(start, p=p):
            product = product_rows(loader(far_in[p], rows_of(p), start), slices)
            out = flat_rows(psend[p])
            for r in range(2):
                for k in range(3):
                    for q in range(2):
                        out[(r * 3 + k) * 2 + q, pl.ds(start, SUBLANES), :] = product[r][k][q]

        each_group(p, far)
        if p == 0:

            @pl.when(ta == 1)
            def _():
                pl.semaphore_wait(beside, 1)

        swap(p).start()

    def do_near(p):
        if WALK.index(p) % 2 == 0:
            first, length = pairs[WALK.index(p) // 2]
            total(near_pool.at[pl.ds(first * depth, length * depth)], in_sem.at[count + WALK.index(p) // 2]).wait()

        def near(start, p=p):
            product = product_rows(loader(near_in[p], rows_of(p), start), slices)
            product.append(cross_conj(product[0], product[1]))
            for r in range(3):
                for k in range(3):
                    for q in range(2):
                        held[p][(r * 3 + k) * 2 + q, pl.ds(start, SUBLANES), :] = product[r][k][q]

        each_group(p, near)

    def scatter(p, q, place):
        return pltpu.make_async_remote_copy(
            src_ref=tr[p].at[q],
            dst_ref=gath[p].at[gx],
            send_sem=sent,
            recv_sem=r2.at[jnp.where(gx < early, 0, 2) + p % 2],
            device_id={"ta": 1, "gx": place},
            device_id_type=MESH,
        )

    def hand_over(p, q):
        place = home(p // 2, q, ta)
        itself = jnp.logical_and(ta == 1, place == gx)

        @pl.when(jnp.logical_not(itself))
        def _():
            scatter(p, q, place).start()

        @pl.when(itself)
        def _():
            gath[p][gx] = tr[p][q]

    upper = jnp.where(gx < gx_n // 2, 1, 0)

    def do_trace(p):
        swap(p).wait_recv()

        def trace(start, p=p):
            theirs_ref = flat_rows(precv[p])

            def entry(ref, r, k):
                return tuple(ref[(r * 3 + k) * 2 + q, pl.ds(start, SUBLANES), :] for q in range(2))

            ours = [[entry(held[p], r, k) for k in range(3)] for r in range(3)]
            theirs = [[entry(theirs_ref, r, k) for k in range(3)] for r in range(2)]
            pair = trace_of_product(ours, theirs)
            flat_loop = loop_refs[p].reshape(rows_of(p) * 2, LANES)
            flat_tr = flat_rows(tr[p])
            for q in range(2):
                flat_loop[pl.ds(2 * start + q, SUBLANES, stride=2), :] = pair[q]
                flat_tr[q, pl.ds(start, SUBLANES), :] = pair[q]

        each_group(p, trace)
        at = WALK.index(p)
        def release(turn):
            hand_over(WALK[turn], upper)
            hand_over(WALK[turn], 1 - upper)

        @pl.when(jnp.logical_not(jnp.logical_or(is_first, is_slow)))
        def _():
            if at == 0:
                clear()
            release(at)

        if at >= 2:

            @pl.when(is_slow)
            def _():
                if at == 2:
                    clear()
                    release(0)
                    release(1)
                release(at)

    for work in (do_far, do_near, do_trace):
        for p in WALK:
            work(p)

    @pl.when(is_first)
    def _():
        for h in reversed(range(PARTS)):
            for q in range(2):
                pl.semaphore_wait(ready.at[h * 2 + q], 1)
                for k in range(2):
                    hand_over(h * 2 + k, q)

    def report(core, j, slot):
        return pltpu.make_async_remote_copy(
            src_ref=gram.at[:, pl.ds(j * slab, slab)],
            dst_ref=part.at[slot],
            send_sem=sent,
            recv_sem=r3,
            device_id={"ta": core, "gx": j},
            device_id_type=MESH,
        )

    flat_gram = gram.reshape(lane_tiles, wide, LANES)

    def contract(k, low, high, width):
        tiles = split[k][1]
        flat_gath = gath[k].reshape(gx_n * rows_of(k), LANES)
        tops, bottoms = [], []
        for i in range(tiles):
            values = flat_gath[pl.ds(i, width, stride=tiles), :]
            top = values.astype(jnp.bfloat16)
            tops.append(top)
            bottoms.append((values - top.astype(jnp.float32)).astype(jnp.bfloat16))
        top = jnp.concatenate(tops, axis=1)
        bottom = jnp.concatenate(bottoms, axis=1)

        def dot(a, b):
            return lax.dot_general(a, b, (((1,), (1,)), ((), ())), preferred_element_type=jnp.float32)

        return dot(top[low:high], top) + (dot(top[low:high], bottom) + dot(bottom[low:high], top))

    def place_rows(product, low, high, width):
        padding = lane_tiles * LANES - width
        if padding:
            product = jnp.concatenate([product, jnp.zeros((high - low, padding), jnp.float32)], axis=1)
        for i in range(lane_tiles):
            flat_gram[i, low:high] = product[:, i * LANES : (i + 1) * LANES]

    def tell(j, carry):
        for core in range(2):

            @pl.when(jnp.logical_or(core != ta, j != gx))
            def _():
                report(core, j, mine).start()

        return carry

    first_rows = planes * near_targets

    def reduce_part(h):
        pieces = (2 * h, 2 * h + 1)
        products = []
        for k, p in enumerate(pieces):
            @pl.when(from_core == 0)
            def _():
                total(gath[p].at[pl.ds(0, early)], r2.at[k]).wait()

            @pl.when(from_core == 1)
            def _():
                total(gath[p].at[pl.ds(0, early - 1)], r2.at[k]).wait()

            products.append(contract(p, 0, first_rows, planes * early))
        place_rows(products[0] + products[1], 0, first_rows, planes * early)
        lax.fori_loop(0, near_targets, tell, 0)
        products = []
        for k, p in enumerate(pieces):
            total(gath[p].at[pl.ds(0, gx_n - early)], r2.at[2 + k]).wait()
            products.append(contract(p, first_rows, wide, wide))
        place_rows(products[0] + products[1], first_rows, wide, wide)
        lax.fori_loop(near_targets, gx_n, tell, 0)

    for h in range(PARTS):

        @pl.when(jnp.logical_and(is_reducer, from_part == h))
        def _():
            reduce_part(h)

    @pl.when(is_reducer)
    def _():
        part[mine] = gram[:, pl.ds(gx * slab, slab)]
        total(part.at[pl.ds(0, REDUCERS - 1)], r3).wait()

    @pl.when(jnp.logical_not(is_reducer))
    def _():
        total(part, r3).wait()

    flat_part = part.reshape(REDUCERS, lane_tiles, planes, LANES)
    chunks = []
    for i in range(lane_tiles):
        chunk = flat_part[0, i]
        for slot in range(1, REDUCERS):
            chunk = chunk + flat_part[slot, i]
        chunks.append(chunk)
    summed = chunks[0] if lane_tiles == 1 else jnp.concatenate(chunks, axis=1)
    extra = -planes % SUBLANES
    if extra:
        summed = jnp.concatenate([summed, jnp.zeros((extra, summed.shape[1]), jnp.float32)], axis=0)
    corr_ref[...] = summed

    def drain(length):
        while length:
            some = min(length, near_pool.shape[0])
            total(near_pool.at[pl.ds(0, some)], sent).wait()
            length -= some

    shared = 7 * planes * half
    reports = (2 * gx_n - 1) * slab * lane_tiles
    inside = jnp.logical_and(is_reducer, from_core == 1)

    @pl.when(jnp.logical_not(is_reducer))
    def _():
        drain(shared)

    @pl.when(jnp.logical_and(is_reducer, from_core == 0))
    def _():
        drain(shared + reports)

    for h in range(PARTS):

        @pl.when(jnp.logical_and(inside, from_part == h))
        def _():
            drain(shared + reports - (rows_of(2 * h) + rows_of(2 * h + 1)) // 2)


def place_outputs(dims, split, *refs):
    planes, sites, gx_n, longest = dims[1:]
    wide = planes * gx_n
    count = len(split)
    loop_in, (total_ref, loop_out, corr_out, corr, semaphores) = refs[:count], refs[count:]
    gx = lax.axis_index("gx")
    copies = [
        pltpu.make_async_copy(loop_in[p], loop_out.at[:, pl.ds(start, n)], semaphores.at[p])
        for p, (start, n) in enumerate(split)
    ]
    for copy in copies:
        copy.start()
    summed = total_ref[...]
    width = summed.shape[1]
    row_index = lax.broadcasted_iota(jnp.int32, summed.shape, 0)
    column = lax.broadcasted_iota(jnp.int32, summed.shape, 1)
    answer = jnp.zeros(summed.shape, jnp.float32)
    for i in range(planes):
        start = gx * planes + i
        ahead = pltpu.roll(summed, (width - start) % width, 1)
        if width == wide:
            value = ahead
        else:
            around = pltpu.roll(summed, (width + wide - start) % width, 1)
            value = jnp.where(column + start < wide, ahead, around)
        answer = jnp.where(row_index == i, value, answer)
    corr[...] = answer[0:planes, 0 : longest + 1] / sites
    last = pltpu.make_async_copy(corr, corr_out, semaphores.at[count])
    last.start()
    for copy in copies:
        copy.wait()
    last.wait()


def per_device(gx_n, time_links):
    slices, _, _, _, planes, sites = time_links.shape
    blocks = sites // LANES
    held = time_links.transpose(0, 2, 3, 4, 1, 5)
    held = held.reshape(slices, 3, 3, planes, 2, blocks, LANES).swapaxes(4, 5)
    half = blocks // 2
    less = half // PARTS
    split = []
    for start, tiles in ((0, less), (less, half - less)):
        lead = tiles - tiles // 2
        split += [(start, lead), (start + lead, tiles - lead)]
    longest = planes * (gx_n // 2)
    wide = planes * gx_n
    lane_tiles = -(-wide // LANES)
    dims = (slices, planes, sites, gx_n, longest)
    dma = pltpu.SemaphoreType.DMA
    regular = pltpu.SemaphoreType.REGULAR
    f32 = jnp.float32
    count = len(split)
    links = [
        pltpu.VMEM((2 * slices, 3, planes, n, 2, LANES), f32)
        for _, n in split
    ]
    links.append(pltpu.VMEM((2 * slices * 3 * planes * half, 2, LANES), f32))
    swaps = [pltpu.VMEM((12, planes * n // 2, 2, LANES), f32) for _, n in split]
    scratch = links + swaps + swaps
    scratch += [pltpu.VMEM((18, planes * n, LANES), f32) for _, n in split]
    scratch += [pltpu.VMEM((2, planes * n // 2, 2, LANES), f32) for _, n in split]
    scratch += [pltpu.VMEM((gx_n, planes * n // 2, 2, LANES), f32) for _, n in split]
    scratch += [
        pltpu.VMEM((lane_tiles, wide // 2, 2, LANES), f32),
        pltpu.VMEM((REDUCERS, lane_tiles, planes // 2, 2, LANES), f32),
        dma((count + count // 2,)),
        dma,
        dma((count,)),
        dma((4,)),
        dma,
        regular((2 * PARTS,)),
        regular,
    ]
    in_vmem = pl.BlockSpec(memory_space=pltpu.VMEM)
    results = pl.pallas_call(
        functools.partial(kernel, dims, split),
        out_shape=[pltpu.VMEM((planes, n, 2, LANES), f32) for _, n in split]
        + [pltpu.VMEM((-(-planes // SUBLANES) * SUBLANES, lane_tiles * LANES), f32)],
        in_specs=[pl.BlockSpec(memory_space=pl.ANY)],
        out_specs=[in_vmem] * (count + 1),
        scratch_shapes=scratch,
        compiler_params=pltpu.CompilerParams(collective_id=0, has_side_effects=True),
    )(held)
    results = [pltpu.with_memory_space_constraint(r, pltpu.VMEM) for r in results]
    loops, correlator = pl.pallas_call(
        functools.partial(place_outputs, dims, split),
        out_shape=(
            jax.ShapeDtypeStruct((planes, half, 2, LANES), f32),
            jax.ShapeDtypeStruct((planes, longest + 1), f32),
        ),
        in_specs=[in_vmem] * (count + 1),
        out_specs=(pl.BlockSpec(memory_space=pl.ANY),) * 2,
        scratch_shapes=[pltpu.VMEM((planes, longest + 1), f32), dma((count + 1,))],
    )(*results)
    return loops.swapaxes(1, 2).reshape(planes, 2, sites // 2), correlator


def solution(mesh):
    in_specs = (P("ta", None, None, None, "gx", None),)
    out_specs = (P("gx", None, "ta"), P("gx", None))
    return jax.shard_map(
        functools.partial(per_device, mesh.shape["gx"]),
        mesh=mesh,
        in_specs=in_specs,
        out_specs=out_specs,
        check_vma=False,
    )
```

time: 15.7 us -> 15.1 us (0.962)
  Pallas kernels: 14.9 us -> 14.4 us
    pallas_call x1, Pallas kernels: 14.2 us -> 13.6 us  [per_device(): pl.pallas_call(functools.partial(kernel, dims, split), out_shape=[pltpu.V...]
where the time goes in v3:
time: 15.1 us; the launch traced here: 15 us
  Pallas kernels  14.4 us (95%)
  between operations  0.64 us (4%)
    pallas_call x1, Pallas kernels, per_device(): pl.pallas_call(functools.partial(kernel, dims, split), out_shape=[pltpu.V...  13.6 us
    pallas_call x1, Pallas kernels, per_device(): pl.pallas_call(functools.partial(place_outputs, dims, split), out_shape=(...  0.73 us

profile of v3, /device:TPU:0, one launch (start us, length us, event | category | flops | bytes accessed | tf_op | source)
XLA Modules:
  0.0 15.0 jit_solution(8170247626461220345)
XLA Ops:
  0.6 13.6 %shard_map.30 = (f32[6,5,2,128]{3,2,1,0:T(2,128)S(1)}, f32[6,4,2,128]{3,2,1,0:T(2,128)S(1)}, f32[6,5,2,128]{3,2,1,0:T(2,128)S(1)}, f32[6,4,2,128]{3,2,1,0:T(2,128)S(1)}, f32[8,128]{1,0:T(8,128)S(1)}) custom-call(f32[3,3,3,6,36,2,128]{6,5,4,3,2,1,0:T(2,128)} %bitcast.8), custom_call_target="tpu_custom_call" | custom-call | tf_op jit(solution)/shard_map/pallas_call | solution.py:533
  14.3 0.7 %shard_map.31 = (f32[6,18,2,128]{3,2,1,0:T(2,128)}, f32[6,49]{1,0:T(8,128)}) custom-call(f32[6,5,2,128]{3,2,1,0:T(2,128)S(1)} %get-tuple-element.9.refs_0_, f32[6,4,2,128]{3,2,1,0:T(2,128)S(1)} %get-tuple-element.10.refs_1_, f32[6,5,2,128]{3,2,1,0:T(2,128)S(1)} %get-tuple-element.11.refs_2_, f32[6,4,2,128]{3,2,1,0:T(2,128)S(1)} %get-tuple-element.12.refs_3_, ...), custom_call_target="tpu_custom_call" | custom-call | tf_op jit(solution)/shard_map/pallas_call | solution.py:543

commit v4 on v3

--- a/solution.py
+++ b/solution.py
@@ -107,7 +107,6 @@
     is_first = gx == 0
     is_slow = gx % 2 + gx // 2 % 2 + gx // 4 == 1
 
-    half = sum(n for _, n in split)
     depth = near_pool.shape[0] // half
     near_in = [None] * count
     pairs = []
@@ -197,7 +196,7 @@
             body(begin(p, g))
             return carry
 
-        lax.fori_loop(0, -(-rows_of(p) // SUBLANES), run, 0)
+        lax.fori_loop(0, -(-rows_of(p) // SUBLANES), run, 0, unroll=True)
 
     def loader(ref, rows, start):
         flat = ref.reshape(*ref.shape[:2], rows * 2, LANES)
@@ -301,6 +300,7 @@
 
         each_group(p, trace)
         at = WALK.index(p)
+
         def release(turn):
             hand_over(WALK[turn], upper)
             hand_over(WALK[turn], 1 - upper)

time: 15.1 us -> 15.1 us (level)
  no operation moved by 1% of the time
where the time goes in v4:
time: 15.1 us; the launch traced here: 14.9 us
  Pallas kernels  14.3 us (95%)
  between operations  0.64 us (4%)
    pallas_call x1, Pallas kernels, per_device(): pl.pallas_call(functools.partial(kernel, dims, split), out_shape=[pltpu.V...  13.6 us
    pallas_call x1, Pallas kernels, per_device(): pl.pallas_call(functools.partial(place_outputs, dims, split), out_shape=(...  0.73 us

profile of v4, /device:TPU:0, one launch (start us, length us, event | category | flops | bytes accessed | tf_op | source)
XLA Modules:
  0.0 14.9 jit_solution(13899191928754120484)
XLA Ops:
  0.6 13.6 %shard_map.30 = (f32[6,5,2,128]{3,2,1,0:T(2,128)S(1)}, f32[6,4,2,128]{3,2,1,0:T(2,128)S(1)}, f32[6,5,2,128]{3,2,1,0:T(2,128)S(1)}, f32[6,4,2,128]{3,2,1,0:T(2,128)S(1)}, f32[8,128]{1,0:T(8,128)S(1)}) custom-call(f32[3,3,3,6,36,2,128]{6,5,4,3,2,1,0:T(2,128)} %bitcast.8), custom_call_target="tpu_custom_call" | custom-call | tf_op jit(solution)/shard_map/pallas_call | solution.py:533
  14.2 0.7 %shard_map.31 = (f32[6,18,2,128]{3,2,1,0:T(2,128)}, f32[6,49]{1,0:T(8,128)}) custom-call(f32[6,5,2,128]{3,2,1,0:T(2,128)S(1)} %get-tuple-element.9.refs_0_, f32[6,4,2,128]{3,2,1,0:T(2,128)S(1)} %get-tuple-element.10.refs_1_, f32[6,5,2,128]{3,2,1,0:T(2,128)S(1)} %get-tuple-element.11.refs_2_, f32[6,4,2,128]{3,2,1,0:T(2,128)S(1)} %get-tuple-element.12.refs_3_, ...), custom_call_target="tpu_custom_call" | custom-call | tf_op jit(solution)/shard_map/pallas_call | solution.py:543
